TPU v7x, 32 devices: a whole 2x2x4 slice. The times are simulated.
32 devices in a mesh: expert: 2 (over x), dp: 16 (over z, y, core).
Axes of the slice: x: 2, y: 2, z: 4, core: 2. Of those that a mesh axis runs over, the one named last changes fastest.
Arguments:
- features: bfloat16 [4096, 512], P(('expert', 'dp')), may hold values from -31 to 31
- gradients: bfloat16 [4096, 512], P(('expert', 'dp')), may hold values from -31 to 31
- route_ids: int32 [4096, 2], P(('expert', 'dp')), may hold values from 0 to 7, all different within a row; in each aligned block of 128 rows (0 to 127, 128 to 255, ...) at most 64 rows name the same one
- gate_share: float32 [4096], P(('expert', 'dp')), may hold values from 0.5 to 0.95
- token_mask: int32 [4096], P(('expert', 'dp')), may hold values 0 or 1
- damping: float32 [8, 2, 1], P('expert'), may hold values from 0.5 to 2
Outputs:
- act_inverse: float32 [8, 1, 512, 512], P(None, None, 'dp')
- grad_inverse: float32 [8, 1, 512, 512], P(None, None, 'dp')
Inputs may be any that keep to these rules, and one draw needn't show every extreme that they name: `route_ids`: each token names two different experts. Among the 128 tokens of one device no expert is named by more than 64 tokens, a bound that some block reaches.
All inputs are finite; a program needn't handle non-finite values. Where the computation divides by a largest or mean magnitude, that divisor is 1e-20 or more. No bound on the sum of `token_mask` on one device may be relied on, other than what follows from the above.
Results may differ from a plain program's by a relative error of at most 0.0003.
Values may be sent and summed in bfloat16 or wider, within the bound.
No kernel may reach another device: no remote copies, remote signals or barrier semaphores. Data moves between devices by JAX's collectives and lax.ppermute only.
A program may use at most 64 MiB of HBM per device.

v0:
```python
import jax
import jax.numpy as jnp
from jax import lax
from jax.sharding import PartitionSpec as P

EXPERTS = 8
TOP = 2
BLOCK = 512
NBLK = 1
CAP = 64
WIDTH = 512


def slot_table(route_ids, capacity):
    pair_experts = route_ids.reshape(-1)
    onehot = (pair_experts[:, None] == jnp.arange(EXPERTS, dtype=jnp.int32)[None, :]).astype(
        jnp.int32
    )
    running = jnp.cumsum(onehot, axis=0)
    position = jnp.sum(onehot * running, axis=1) - 1
    target = pair_experts * capacity + position
    sources = jnp.arange(1, pair_experts.shape[0] + 1, dtype=jnp.int32)
    return jnp.zeros((EXPERTS * capacity,), jnp.int32).at[target].set(sources)


def newton_rows(rows_now, matrix, whole_now):
    left_product = jnp.einsum("eirk,eikc->eirc", rows_now, matrix, precision=lax.Precision.HIGHEST)
    return 2.0 * rows_now - jnp.einsum(
        "eirk,eikc->eirc", left_product, whole_now, precision=lax.Precision.HIGHEST
    )


def first_iterate(matrix, identity, inverse_bound):
    bound_scale = inverse_bound[:, :, None, None]
    return 2.0 * bound_scale * identity - bound_scale * bound_scale * matrix


def on_device(features, gradients, route_ids, gate_share, token_mask, damping):
    tokens_here = features.shape[0]
    capacity = CAP
    blocks = 2 * NBLK
    kept_mask = token_mask.astype(jnp.float32)
    weight_pair = jnp.stack([gate_share, 1.0 - gate_share], axis=1) * kept_mask[:, None]
    kept_rows = features * token_mask.astype(jnp.bfloat16)[:, None]
    pair_grads = (gradients[:, None, :].astype(jnp.float32) * weight_pair[:, :, None]).astype(
        jnp.bfloat16
    )
    repeated = jnp.broadcast_to(kept_rows[:, None, :], pair_grads.shape)
    pair_rows = jnp.concatenate([repeated, pair_grads], axis=2).reshape(
        tokens_here * TOP, 2 * WIDTH
    )
    padded = jnp.concatenate([jnp.zeros((1, 2 * WIDTH), jnp.bfloat16), pair_rows], axis=0)
    buffer = jnp.take(padded, slot_table(route_ids, capacity), axis=0).reshape(
        EXPERTS, capacity, blocks, BLOCK
    )
    load_inverse = 1.0 / (
        tokens_here * lax.axis_size("expert") * lax.axis_size("dp") * TOP / EXPERTS
    )
    received = lax.all_to_all(buffer, "expert", split_axis=0, concat_axis=1, tiled=True)
    gram_blocks = (
        jnp.einsum("erib,eric->eibc", received, received, preferred_element_type=jnp.float32)
        * load_inverse
    )
    damping_flat = damping.reshape(damping.shape[0], blocks)[:, :, None, None]
    rows_share = BLOCK // lax.axis_size("dp")
    row_start = lax.axis_index("dp") * rows_share
    identity = jnp.eye(BLOCK, dtype=jnp.float32)
    summed = lax.psum(gram_blocks, "dp")
    matrix = summed + damping_flat * identity
    largest_sum = jnp.max(jnp.sum(jnp.abs(matrix), axis=3), axis=2)
    inverse_bound = 1.0 / largest_sum
    iterate_one = first_iterate(matrix, identity, inverse_bound)
    iterate_two = newton_rows(iterate_one, matrix, iterate_one)
    second_rows = lax.dynamic_slice_in_dim(iterate_two, row_start, rows_share, 2)
    third_rows = newton_rows(second_rows, matrix, iterate_two)
    act_rows = third_rows[:, :NBLK]
    grad_rows = third_rows[:, NBLK:]
    act_inverse, grad_inverse = (
        lax.all_gather(act_rows, "expert", axis=0, tiled=True),
        lax.all_gather(grad_rows, "expert", axis=0, tiled=True),
    )
    return (act_inverse, grad_inverse)


def solution(mesh):
    placed = (
        P(("expert", "dp"), None),
        P(("expert", "dp"), None),
        P(("expert", "dp"), None),
        P(("expert", "dp")),
        P(("expert", "dp")),
        P("expert", None, None),
    )
    return jax.shard_map(
        on_device,
        mesh=mesh,
        in_specs=placed,
        out_specs=(P(None, None, "dp", None), P(None, None, "dp", None)),
        check_vma=False,
    )
```

profile of v0, /device:TPU:0, one launch (start us, length us, event | category | flops | bytes accessed | tf_op | source)
XLA Modules:
  0.0 298.0 jit_solution(7920612828320791945)
XLA Ops:
  7.2 0.0 all-reduce.3.cloned.1.call-start
  7.2 0.8 copy.37
  8.0 0.1 eq.38
  8.1 0.1 eq.34
  8.3 0.7 broadcast_multiply_fusion.3
  9.0 0.6 reduce-window.6
  9.6 0.2 slice_reduce_fusion
  9.8 0.1 fusion.18
  9.9 0.1 copy.36
  10.0 0.1 mul.132
  10.2 1.4 scatter_custom_fusion
  11.6 0.7 fusion.25
  12.4 0.1 mul.138
  12.4 0.1 mul.139
  12.6 0.7 subtract_bitcast_fusion
  13.2 0.7 pad_maximum_fusion
  13.9 0.1 copy.39
  14.0 0.1 stack.14
  14.2 1.0 mul.136
  15.2 0.4 mul.137
  15.6 1.0 broadcast_multiply_fusion.1
  16.6 0.1 broadcast_in_dim.36
  16.7 0.1 concatenate.12
  16.8 0.1 multiply_convert_fusion
  17.0 0.1 fusion.16
  17.1 2.1 gather_fusion
  19.2 0.8 gather.7
  20.0 0.1 broadcast_in_dim.19
  20.0 0.2 copy_select_fusion
  20.2 17.7 %all_to_all.18 = bf16[8,64,2,512]{3,1,2,0:T(8,128)(2,1)S(1)} all-to-all(bf16[8,64,2,512]{3,1,2,0:T(8,128)(2,1)S(1)} %copy_select_fusion), channel_id=1, replica_groups=mesh['expert'=2,'dp'=16] {'expert'}, dimensions={0} | all-to-all | bytes 2097152 | tf_op jit(solution)/shard_map/all_to_all | solution.py:59
  38.0 0.1 copy.41
  38.1 0.0 copy-start.2
  38.1 4.5 %broadcast_multiply_fusion = f32[4,2,512,512]{3,2,1,0:T(8,128)} fusion(bf16[4,128,2,512]{3,1,2,0:T(8,128)(2,1)S(1)} %bitcast.23), kind=kOutput, calls=%fused_computation.19 | convolution fusion | flops 538968064 | bytes 9437184 | tf_op jit(solution)/shard_map/erib,eric->eibc/dot_general | solution.py:61
  42.6 0.0 all-reduce.3.cloned.1.call-update
  42.6 0.0 copy-done.2
  42.6 0.1 copy.43
  42.7 0.1 fusion.15
  42.8 170.4 %all-reduce.3.cloned.1.call-done = f32[4,2,512,512]{3,2,1,0:T(8,128)} async-done(((f32[4,2,512,512]{3,2,1,0:T(8,128)}), f32[4,2,512,512]{3,2,1,0:T(8,128)}) %all-reduce.3.cloned.1.call-update) | async-done | bytes 8388624 | tf_op jit(solution)/shard_map/psum | solution.py:68
  213.2 4.6 %abs_reduce_fusion = f32[4,2,512]{2,1,0:T(2,128)S(1)} fusion(f32[4,2,512,512]{3,2,1,0:T(8,128)} %all-reduce.3.cloned.1.call-done, f32[512,512]{1,0:T(8,128)S(1)} %fusion.15, f32[4,2]{1,0:T(4,128)S(1)} %copy.43), kind=kLoop, calls=%fused_computation.6 | loop fusion | flops 8384512 | bytes 9453600 | tf_op jit(solution)/shard_map/reduce_sum | solution.py:70
  217.8 0.1 reduce_max.9
  217.9 0.1 copy.48
  218.0 0.1 copy.45
  218.1 0.1 copy.46
  218.2 0.0 copy-start
  218.2 23.3 %fusion.1 = f32[4,2,512,512]{3,2,1,0:T(8,128)} fusion(f32[4,2,512,512]{3,2,1,0:T(8,128)} %all-reduce.3.cloned.1.call-done, f32[4,2]{1,0:T(4,128)S(1)} %copy.46, f32[4,2]{1,0:T(4,128)S(1)} %copy.45, f32[512,512]{1,0:T(8,128)S(1)} %fusion.15, f32[4,2]{1,0:T(4,128)S(1)} %copy.43), kind=kOutput, calls=%fused_computation.5 | convolution fusion | flops 12899581952 | bytes 17825888 | tf_op jit(solution)/shard_map/eirk,eikc->eirc/dot_general | solution.py:27
  241.5 0.0 copy-done
  241.5 19.9 %multiply_subtract_fusion = f32[4,2,512,512]{3,2,1,0:T(8,128)} fusion(f32[4,2,512,512]{3,2,1,0:T(8,128)} %fusion.1, f32[4,2,512,512]{3,2,1,0:T(8,128)S(1)} %copy-done, f32[4,2]{1,0:T(4,128)S(1)} %copy.46, f32[4,2]{1,0:T(4,128)S(1)} %copy.45, f32[512,512]{1,0:T(8,128)S(1)} %fusion.15, f32[4,2]{1,0:T(4,128)S(1)} %copy.43), kind=kOutput, calls=%fused_computation.2 | convolution fusion | flops 12910067712 | bytes 26214496 | tf_op jit(solution)/shard_map/eirk,eikc->eirc/dot_general | solution.py:28
  261.4 0.0 copy-start.1
  261.4 6.8 %fusion.2 = f32[4,2,32,512]{3,2,1,0:T(8,128)S(1)} fusion(f32[4,2,512,512]{3,2,1,0:T(8,128)S(1)} %copy-done, f32[512,512]{1,0:T(8,128)S(1)} %fusion.15, f32[4,2]{1,0:T(4,128)S(1)} %copy.43, f32[4,2,512,512]{3,2,1,0:T(8,128)} %multiply_subtract_fusion, s32[]{:T(128)S(6)} %select_n.26), kind=kOutput, calls=%fused_computation.8 | convolution fusion | flops 809500672 | bytes 10485796 | tf_op jit(solution)/shard_map/eirk,eikc->eirc/dot_general | solution.py:27
  268.2 0.0 copy-done.1
  268.2 4.9 %convolution_subtract_fusion = f32[4,2,32,512]{3,2,1,0:T(8,128)S(1)} fusion(f32[4,2,32,512]{3,2,1,0:T(8,128)S(1)} %fusion.2, f32[4,2,512,512]{3,2,1,0:T(8,128)S(1)} %copy-done.1, s32[]{:T(128)S(6)} %select_n.26), kind=kOutput, calls=%fused_computation.20 | convolution fusion | flops 805568512 | bytes 9961476 | tf_op jit(solution)/shard_map/eirk,eikc->eirc/dot_general | solution.py:28
  273.1 8.7 %all_gather.6 = f32[8,1,32,512]{3,2,1,0:T(8,128)S(1)} all-gather(f32[4,1,32,512]{3,2,1,0:T(8,128)S(1)} %get-tuple-element.3), channel_id=1, replica_groups=mesh['expert'=2,'dp'=16] {'expert'}, dimensions={0}, use_global_device_ids=true | all-gather | bytes 786432 | tf_op jit(solution)/shard_map/all_gather | solution.py:79
  281.8 7.8 %all_gather.7 = f32[8,1,32,512]{3,2,1,0:T(8,128)S(1)} all-gather(f32[4,1,32,512]{3,2,1,0:T(8,128)S(1)} %get-tuple-element.2), channel_id=1, replica_groups=mesh['expert'=2,'dp'=16] {'expert'}, dimensions={0}, use_global_device_ids=true | all-gather | bytes 786432 | tf_op jit(solution)/shard_map/all_gather | solution.py:80
  289.6 0.8 copy.53
  290.4 0.8 copy.54
  (12 shorter events, 0.1 us)
Async XLA Ops:
  7.2 206.0 %all-reduce.3.cloned.1.call-start = ((), (), s32[]{:S(2)}) async-start(), calls=%async_computation.1 | async-start | bytes 16777216 | tf_op jit(solution)/shard_map/psum | solution.py:68
  38.1 4.5 %copy-start.2 = (f32[4,2,1]{0,2,1:T(1,128)S(1)}, f32[4,2,1]{0,2,1:T(1,128)}, u32[]{:S(2)}) copy-start(f32[4,2,1]{0,2,1:T(1,128)} %param.11) | copy-start | bytes 100
  218.2 23.3 %copy-start = (f32[4,2,512,512]{3,2,1,0:T(8,128)S(1)}, f32[4,2,512,512]{3,2,1,0:T(8,128)}, u32[]{:S(2)}) copy-start(f32[4,2,512,512]{3,2,1,0:T(8,128)} %all-reduce.3.cloned.1.call-done) | copy-start | bytes 25165828
  261.4 6.8 %copy-start.1 = (f32[4,2,512,512]{3,2,1,0:T(8,128)S(1)}, f32[4,2,512,512]{3,2,1,0:T(8,128)}, u32[]{:S(2)}) copy-start(f32[4,2,512,512]{3,2,1,0:T(8,128)} %multiply_subtract_fusion) | copy-start | bytes 25165828
Sparse Core Ops, SparseCore 0:
  42.7 170.4 all-reduce.2
where the time goes:
time: 298 us
  waiting for transfers between devices  170 us (57%)
  matrix products  59.3 us (20%)
  blocking collectives  34.2 us (11%)
  between operations  14.2 us (5%)
  local copies, waits for them, and re-layouts  10.1 us (3%)
  other arithmetic  9.73 us (3%)
    psum x1, waiting for transfers between devices, on_device(): summed = lax.psum(gram_blocks, 'dp')  170 us
    dot_general x2, matrix products, newton_rows(): jnp.einsum('eirk,eikc->eirc', rows_now, matrix, precision=lax.Precision.H...  30.1 us
    dot_general x2, matrix products, newton_rows(): jnp.einsum('eirk,eikc->eirc', left_product, whole_now, precision=lax.Prec...  24.7 us
    all_to_all x1, blocking collectives, on_device(): lax.all_to_all(buffer, 'expert', split_axis=0, concat_axis=1, tiled=True)  17.7 us
    all_gather x1, blocking collectives, on_device(): lax.all_gather(act_rows, 'expert', axis=0, tiled=True)  8.67 us
    all_gather x1, blocking collectives, on_device(): lax.all_gather(grad_rows, 'expert', axis=0, tiled=True)  7.79 us
  transfers between devices with their start and end apart: 1, of which 1 were waited for; matrix products, arithmetic and copies ran while one was open for 0% of the time, Pallas kernels for 0%

commit v1 on v0

--- a/solution.py
+++ b/solution.py
@@ -1,6 +1,10 @@
+import functools
+
 import jax
 import jax.numpy as jnp
 from jax import lax
+from jax.experimental import pallas as pl
+from jax.experimental.pallas import tpu as pltpu
 from jax.sharding import PartitionSpec as P
 
 EXPERTS = 8
@@ -9,6 +13,148 @@
 NBLK = 1
 CAP = 64
 WIDTH = 512
+FACTORS = 2 * NBLK
+MATRICES = EXPERTS * FACTORS
+AXES = ("expert", "dp")
+
+
+def whole(*shape):
+    return pl.BlockSpec(memory_space=pltpu.VMEM)
+
+
+def pack_kernel(features, gradients, routes, share, mask, out):
+    tokens = features.shape[0]
+    first, second = routes[0:1, :], routes[1:2, :]
+    kept = mask[...] > 0
+    expert = lax.broadcasted_iota(jnp.int32, (EXPERTS, tokens), 0)
+    is_first, is_second = expert == first, expert == second
+    member = jnp.where(is_first | is_second, 1.0, 0.0).astype(jnp.bfloat16)
+    earlier = lax.broadcasted_iota(jnp.int32, (tokens, tokens), 0) < lax.broadcasted_iota(
+        jnp.int32, (tokens, tokens), 1
+    )
+    position = jnp.dot(
+        member,
+        jnp.where(earlier, 1.0, 0.0).astype(jnp.bfloat16),
+        preferred_element_type=jnp.float32,
+    )
+
+    def target(chosen, ids):
+        place = jnp.sum(jnp.where(chosen, position, 0.0), axis=0, keepdims=True)
+        return ids * CAP + place.astype(jnp.int32)
+
+    slot = lax.broadcasted_iota(jnp.int32, (EXPERTS * CAP, tokens), 0)
+    pick_first = slot == target(is_first, first)
+    pick_second = slot == target(is_second, second)
+    pick = jnp.where((pick_first | pick_second) & kept, 1.0, 0.0).astype(jnp.bfloat16)
+    rows = jnp.dot(pick, features[...], preferred_element_type=jnp.float32)
+    out[:, 0] = rows.astype(jnp.bfloat16).reshape(EXPERTS, CAP, WIDTH)
+
+    kept_mask = mask[...].astype(jnp.float32)
+    wide = gradients[...].astype(jnp.float32)
+
+    def weighted(weight):
+        column = jnp.transpose(jnp.broadcast_to(weight * kept_mask, (tokens, tokens)))
+        column = jnp.concatenate([column] * (WIDTH // tokens), axis=1)
+        return (wide * column).astype(jnp.bfloat16)
+
+    pairs = jnp.concatenate([weighted(share[...]), weighted(1.0 - share[...])], axis=0)
+    picks = jnp.concatenate(
+        [
+            jnp.where(pick_first, 1.0, 0.0).astype(jnp.bfloat16),
+            jnp.where(pick_second, 1.0, 0.0).astype(jnp.bfloat16),
+        ],
+        axis=1,
+    )
+    rows = jnp.dot(picks, pairs, preferred_element_type=jnp.float32)
+    out[:, 1] = rows.astype(jnp.bfloat16).reshape(EXPERTS, CAP, WIDTH)
+
+
+def gram_kernel(rows, out):
+    out[...] = lax.dot_general(
+        rows[...], rows[...], (((0,), (0,)), ((), ())), preferred_element_type=jnp.float32
+    )
+
+
+def split(value):
+    high = value.astype(jnp.bfloat16)
+    return high, (value - high.astype(jnp.float32)).astype(jnp.bfloat16)
+
+
+def product(left, right):
+    (left_high, left_low), (right_high, right_low) = left, right
+
+    def dot(a, b):
+        return jnp.dot(a, b, preferred_element_type=jnp.float32)
+
+    return dot(left_high, right_high) + (dot(left_high, right_low) + dot(left_low, right_high))
+
+
+def newton_kernel(load_inverse, owners, shards, damping, mine, other, out):
+    core = lax.rem(lax.axis_index("dp"), owners)
+    place = lax.broadcasted_iota(jnp.int32, (BLOCK, BLOCK), 0)
+    identity = jnp.where(place == lax.broadcasted_iota(jnp.int32, (BLOCK, BLOCK), 1), 1.0, 0.0)
+    matrix = (mine[...] + other[...]) * load_inverse + damping[0] * identity
+    bound = jnp.max(jnp.sum(jnp.abs(matrix), axis=0, keepdims=True), axis=1, keepdims=True)
+    scale = 1.0 / bound
+    error = identity - scale * matrix
+    parts = split(error)
+    square = split(product(parts, parts))
+    start = (identity + error).reshape(shards, owners, BLOCK // (shards * owners), BLOCK)
+    rows = start[:, 0]
+    for turn in range(1, owners):
+        rows = jnp.where(core == turn, start[:, turn], rows)
+    rows = rows.reshape(BLOCK // owners, BLOCK)
+    rows = rows + product(split(rows), square)
+    last = rows + product(split(product(split(rows), square)), square)
+    last = scale * last
+    for copy in range(out.shape[0]):
+        out[copy] = last
+
+
+def owned(features, gradients, route_ids, gate_share, token_mask, damping):
+    tokens = features.shape[0]
+    experts_axis, shards = lax.axis_size("expert"), lax.axis_size("dp")
+    devices = experts_axis * shards
+    owners = devices // MATRICES
+    load_inverse = 1.0 / (tokens * devices * TOP / EXPERTS)
+    spec = whole()
+    packed = pl.pallas_call(
+        pack_kernel,
+        out_shape=jax.ShapeDtypeStruct((EXPERTS, FACTORS, CAP, WIDTH), jnp.bfloat16),
+        in_specs=[spec] * 5,
+        out_specs=spec,
+        name="pack",
+    )(
+        features,
+        gradients,
+        route_ids.T,
+        gate_share.reshape(1, tokens),
+        token_mask.reshape(1, tokens),
+    )
+    packed = packed.reshape(MATRICES * CAP, WIDTH)
+    received = lax.all_to_all(packed, AXES, split_axis=0, concat_axis=0, tiled=True)
+    mine = pl.pallas_call(
+        gram_kernel,
+        out_shape=jax.ShapeDtypeStruct((BLOCK, BLOCK), jnp.float32),
+        in_specs=[spec],
+        out_specs=spec,
+        name="gram",
+    )(received)
+    other = lax.ppermute(mine, "dp", [(i, i ^ 1) for i in range(shards)])
+    own_damping = lax.dynamic_slice_in_dim(
+        damping.reshape(-1), lax.axis_index("dp") // owners, 1, 0
+    )
+    rows = pl.pallas_call(
+        functools.partial(newton_kernel, load_inverse, owners, shards),
+        out_shape=jax.ShapeDtypeStruct((experts_axis, BLOCK // owners, BLOCK), jnp.float32),
+        in_specs=[pl.BlockSpec(memory_space=pltpu.SMEM), spec, spec],
+        out_specs=spec,
+        name="newton",
+    )(own_damping, mine, other)
+    rows = rows.reshape(experts_axis * BLOCK // owners, BLOCK)
+    gathered = lax.all_to_all(rows, AXES, split_axis=0, concat_axis=0, tiled=True)
+    gathered = gathered.reshape(EXPERTS, FACTORS, NBLK, BLOCK // shards, BLOCK)
+    return gathered[:, 0], gathered[:, 1]
 
 
 def slot_table(route_ids, capacity):
@@ -35,7 +181,7 @@
     return 2.0 * bound_scale * identity - bound_scale * bound_scale * matrix
 
 
-def on_device(features, gradients, route_ids, gate_share, token_mask, damping):
+def shared(features, gradients, route_ids, gate_share, token_mask, damping):
     tokens_here = features.shape[0]
     capacity = CAP
     blocks = 2 * NBLK
@@ -75,11 +221,10 @@
     third_rows = newton_rows(second_rows, matrix, iterate_two)
     act_rows = third_rows[:, :NBLK]
     grad_rows = third_rows[:, NBLK:]
-    act_inverse, grad_inverse = (
+    return (
         lax.all_gather(act_rows, "expert", axis=0, tiled=True),
         lax.all_gather(grad_rows, "expert", axis=0, tiled=True),
     )
-    return (act_inverse, grad_inverse)
 
 
 def solution(mesh):
@@ -91,8 +236,9 @@
         P(("expert", "dp")),
         P("expert", None, None),
     )
+    paired = mesh.shape["expert"] * mesh.shape["dp"] == 2 * MATRICES
     return jax.shard_map(
-        on_device,
+        owned if paired else shared,
         mesh=mesh,
         in_specs=placed,
         out_specs=(P(None, None, "dp", None), P(None, None, "dp", None)),

time: 298 us -> 82 us (0.28)
  waiting for transfers between devices: 170 us -> 1.42 us
  matrix products: 59.3 us -> 0 us
  blocking collectives: 34.2 us -> 64.4 us
  between operations: 14.2 us -> 0.64 us
  Pallas kernels: 0 us -> 11.6 us
  other arithmetic: 9.73 us -> 0 us
  local copies, waits for them, and re-layouts: 10.1 us -> 3.52 us
    psum x1 -> x0, waiting for transfers between devices: 170 us -> none  [on_device(): summed = lax.psum(gram_blocks, 'dp')]
    dot_general x5 -> x0, matrix products: 59.3 us -> none  [the longest x2 30.1 us: newton_rows(): jnp.einsum('eirk,eikc->eirc', rows_now, matrix, precision=lax.Precision.H...]
    all_to_all x1 -> x2, blocking collectives: 17.7 us -> 64.4 us  [the longest x1 34.6 us: owned(): lax.all_to_all(packed, AXES, split_axis=0, concat_axis=0, tiled=True)]
    all_gather x2 -> x0, blocking collectives: 16.5 us -> none  [the longest x1 8.67 us: on_device(): lax.all_gather(act_rows, 'expert', axis=0, tiled=True)]
    pallas_call x0 -> x3, Pallas kernels: none -> 11.6 us  [the longest x1 6.13 us: owned(): pl.pallas_call(functools.partial(newton_kernel, load_inverse, owners, sha...]
    reduce_sum x2 -> x0, other arithmetic: 4.71 us -> none  [the longest x1 4.62 us: on_device(): largest_sum = jnp.max(jnp.sum(jnp.abs(matrix), axis=3), axis=2)]
  transfers between devices with their start and end apart: 1 -> 1, of which waited for: 1 -> 1; matrix products, arithmetic and copies ran while one was open for 0% -> 1% of each run, Pallas kernels for 0% -> 0%
where the time goes in v1:
time: 82 us; the launch traced here: 81.6 us
  blocking collectives  64.4 us (79%)
  Pallas kernels  11.6 us (14%)
  local copies, waits for them, and re-layouts  3.52 us (4%)
  waiting for transfers between devices  1.42 us (2%)
    all_to_all x1, blocking collectives, owned(): lax.all_to_all(packed, AXES, split_axis=0, concat_axis=0, tiled=True)  34.6 us
    all_to_all x1, blocking collectives, owned(): lax.all_to_all(rows, AXES, split_axis=0, concat_axis=0, tiled=True)  29.8 us
    pallas_call x1, Pallas kernels, owned(): pl.pallas_call(functools.partial(newton_kernel, load_inverse, owners, sha...  6.13 us
    pallas_call x1, Pallas kernels, owned(): pl.pallas_call(gram_kernel, out_shape=jax.ShapeDtypeStruct((BLOCK, BLOCK)...  2.93 us
    unnamed x6, local copies, waits for them, and re-layouts  2.84 us
    pallas_call x1, Pallas kernels, owned(): pl.pallas_call(pack_kernel, out_shape=jax.ShapeDtypeStruct((EXPERTS, FACT...  2.54 us
  transfers between devices with their start and end apart: 1, of which 1 were waited for; matrix products, arithmetic and copies ran while one was open for 1% of the time, Pallas kernels for 0%

profile of v1, /device:TPU:0, one launch (start us, length us, event | category | flops | bytes accessed | tf_op | source)
XLA Modules:
  0.0 81.6 jit_solution(631410017549331471)
XLA Ops:
  0.6 2.5 %pack.1 = bf16[8,2,64,512]{3,2,1,0:T(8,128)(2,1)} custom-call(bf16[128,512]{1,0:T(8,128)(2,1)} %features.1, bf16[128,512]{1,0:T(8,128)(2,1)} %gradients.1, s32[2,128]{1,0:T(2,128)} %bitcast.21, f32[1,128]{1,0:T(1,128)} %bitcast.22, s32[1,128]{1,0:T(1,128)} %bitcast.23), custom_call_target="tpu_custom_call" | custom-call | tf_op jit(solution)/shard_map/pack/pallas_call | solution.py:121
  3.2 34.6 %all_to_all.20 = bf16[32,32,512]{2,1,0:T(8,128)(2,1)} all-to-all(bf16[32,32,512]{2,1,0:T(8,128)(2,1)} %bitcast.17), channel_id=1, replica_groups=mesh['expert'=2,'dp'=16] {'expert','dp'}, dimensions={0} | all-to-all | bytes 2097152 | tf_op jit(solution)/shard_map/all_to_all | solution.py:135
  37.8 2.9 %gram.1.mine = f32[512,512]{1,0:T(8,128)} custom-call(bf16[1024,512]{1,0:T(8,128)(2,1)} %bitcast.20), custom_call_target="tpu_custom_call" | custom-call | tf_op jit(solution)/shard_map/gram/pallas_call | solution.py:136
  40.7 0.0 collective-permute-start
  40.7 0.0 copy-start.1
  40.7 0.7 copy-done.1
  41.4 0.1 copy.9
  41.5 0.1 reshape.25
  41.5 0.6 dynamic_slice.3.damping
  42.1 1.4 %collective-permute-done.other = f32[512,512]{1,0:T(8,128)S(1)} collective-permute-done((f32[512,512]{1,0:T(8,128)}, f32[512,512]{1,0:T(8,128)S(1)}, u32[]{:S(2)}, u32[]{:S(2)}) %collective-permute-start) | collective-permute-done | bytes 1048608 | tf_op jit(solution)/shard_map/ppermute | solution.py:143
  43.6 0.0 copy-start
  43.6 1.0 %copy-done = f32[512,512]{1,0:T(8,128)} copy-done((f32[512,512]{1,0:T(8,128)}, f32[512,512]{1,0:T(8,128)S(1)}, u32[]{:S(2)}) %copy-start) | copy-done | bytes 1048600
  44.6 6.1 %newton.1 = f32[2,256,512]{2,1,0:T(8,128)} custom-call(f32[1]{0:T(128)} %dynamic_slice.3.damping, f32[512,512]{1,0:T(8,128)} %gram.1.mine, f32[512,512]{1,0:T(8,128)} %copy-done), custom_call_target="tpu_custom_call" | custom-call | tf_op jit(solution)/shard_map/newton/pallas_call | solution.py:147
  50.7 29.8 %all_to_all.21 = f32[32,16,512]{2,1,0:T(8,128)S(1)} all-to-all(f32[32,16,512]{2,1,0:T(8,128)} %bitcast.18), channel_id=1, replica_groups=mesh['expert'=2,'dp'=16] {'expert','dp'}, dimensions={0} | all-to-all | bytes 2097152 | tf_op jit(solution)/shard_map/all_to_all | solution.py:155
  80.5 1.1 %slice_bitcast_fusion = (f32[8,1,32,512]{3,2,1,0:T(8,128)}, f32[8,1,32,512]{3,2,1,0:T(8,128)}) fusion(f32[8,2,1,32,512]{4,3,1,0,2:T(8,128)S(1)} %bitcast.19), kind=kLoop, calls=%fused_computation | loop fusion | bytes 2097152
Async XLA Ops:
  40.7 2.9 %collective-permute-start = (f32[512,512]{1,0:T(8,128)}, f32[512,512]{1,0:T(8,128)S(1)}, u32[]{:S(2)}, u32[]{:S(2)}) collective-permute-start(f32[512,512]{1,0:T(8,128)} %gram.1.mine), channel_id=1, source_target_pairs={{0,1},{1,0},{2,3},{3,2},{4,5},{5,4},{6,7},{7,6},{8,9},{9,8},{10,11... | collective-permute-start | bytes 3145736 | tf_op jit(solution)/shard_map/ppermute | solution.py:143
  40.7 0.7 copy-start.1
  43.6 1.0 %copy-start = (f32[512,512]{1,0:T(8,128)}, f32[512,512]{1,0:T(8,128)S(1)}, u32[]{:S(2)}) copy-start(f32[512,512]{1,0:T(8,128)S(1)} %collective-permute-done.other) | copy-start | bytes 3145732

commit v2 on v1

--- a/solution.py
+++ b/solution.py
@@ -15,6 +15,9 @@
 WIDTH = 512
 FACTORS = 2 * NBLK
 MATRICES = EXPERTS * FACTORS
+LANES = 128
+VMEM_GRANT = 16 * 2**20
+SENT_SCALE = 2.0**14
 AXES = ("expert", "dp")
 
 
@@ -90,10 +93,11 @@
 
 
 def newton_kernel(load_inverse, owners, shards, damping, mine, other, out):
-    core = lax.rem(lax.axis_index("dp"), owners)
+    shard = lax.axis_index("dp")
+    core, own = lax.rem(shard, owners), shard // owners
     place = lax.broadcasted_iota(jnp.int32, (BLOCK, BLOCK), 0)
     identity = jnp.where(place == lax.broadcasted_iota(jnp.int32, (BLOCK, BLOCK), 1), 1.0, 0.0)
-    matrix = (mine[...] + other[...]) * load_inverse + damping[0] * identity
+    matrix = (mine[...] + other[...]) * load_inverse + damping[lax.rem(own, FACTORS), own // FACTORS] * identity
     bound = jnp.max(jnp.sum(jnp.abs(matrix), axis=0, keepdims=True), axis=1, keepdims=True)
     scale = 1.0 / bound
     error = identity - scale * matrix
@@ -106,9 +110,58 @@
     rows = rows.reshape(BLOCK // owners, BLOCK)
     rows = rows + product(split(rows), square)
     last = rows + product(split(product(split(rows), square)), square)
-    last = scale * last
-    for copy in range(out.shape[0]):
-        out[copy] = last
+    last = (scale * SENT_SCALE) * last
+    encode(core, shards, owners, last, out)
+
+
+def encode(core, shards, owners, rows, out):
+    share = BLOCK // (shards * owners)
+    out[...] = rows
+    row = lax.broadcasted_iota(jnp.int32, (share, LANES), 0)
+    lane = lax.broadcasted_iota(jnp.int32, (share, LANES), 1)
+    for shard in range(shards):
+        first = shard * share * owners
+        start = first // LANES * LANES
+        tile = rows[shard * share : (shard + 1) * share, start : start + LANES]
+        column = lane - (first - start + core * share)
+        diagonal = jnp.sum(jnp.where(column == row, tile, 0.0), axis=1, keepdims=True)
+        high = diagonal.astype(jnp.bfloat16).astype(jnp.float32)
+        low = diagonal - high
+        tile = jnp.where(column == row, high, tile)
+        tile = jnp.where((column == row - 1) & (row > 0), low, tile)
+        tile = jnp.where((column == 0) & (row == 2), low[0:1, :], tile)
+        out[shard * share : (shard + 1) * share, start : start + LANES] = tile
+
+
+def decode_kernel(owners, share, rows, act, grad):
+    shard = lax.axis_index("dp")
+    per_factor = owners * share
+    first = shard * per_factor
+    start = pl.multiple_of(first // LANES * LANES, LANES)
+    sent = rows[...] * (1.0 / SENT_SCALE)
+    for out, factor in ((act, 0), (grad, 1)):
+        out[:, 0] = sent.reshape(EXPERTS, FACTORS, per_factor, BLOCK)[:, factor]
+    total = rows.shape[0]
+    tile = rows[:, pl.ds(start, LANES)] * (1.0 / SENT_SCALE)
+    place = lax.broadcasted_iota(jnp.int32, (total, LANES), 0)
+    row = lax.rem(place, share)
+    core = lax.rem(place // share, owners)
+    column = lax.broadcasted_iota(jnp.int32, (total, LANES), 1) - (first - start + core * share)
+
+    def moved(down, right):
+        value = tile
+        if down:
+            value = pltpu.roll(value, down % total, 0)
+        if right:
+            value = pltpu.roll(value, right % LANES, 1)
+        return value
+
+    fixed = jnp.where(column == row, tile + jnp.where(row > 0, moved(0, 1), moved(-2, 0)), tile)
+    fixed = jnp.where((column == row - 1) & (row > 0), moved(1, -1), fixed)
+    fixed = jnp.where((column == 0) & (row == 2), moved(2, -2), fixed)
+    fixed = fixed.reshape(EXPERTS, FACTORS, per_factor, LANES)
+    for out, factor in ((act, 0), (grad, 1)):
+        out[:, 0, :, pl.ds(start, LANES)] = fixed[:, factor]
 
 
 def owned(features, gradients, route_ids, gate_share, token_mask, damping):
@@ -120,9 +173,10 @@
     spec = whole()
     packed = pl.pallas_call(
         pack_kernel,
-        out_shape=jax.ShapeDtypeStruct((EXPERTS, FACTORS, CAP, WIDTH), jnp.bfloat16),
+        out_shape=pltpu.VMEM((EXPERTS, FACTORS, CAP, WIDTH), jnp.bfloat16),
         in_specs=[spec] * 5,
         out_specs=spec,
+        compiler_params=pltpu.CompilerParams(vmem_limit_bytes=VMEM_GRANT),
         name="pack",
     )(
         features,
@@ -135,26 +189,33 @@
     received = lax.all_to_all(packed, AXES, split_axis=0, concat_axis=0, tiled=True)
     mine = pl.pallas_call(
         gram_kernel,
-        out_shape=jax.ShapeDtypeStruct((BLOCK, BLOCK), jnp.float32),
+        out_shape=pltpu.VMEM((BLOCK, BLOCK), jnp.float32),
         in_specs=[spec],
         out_specs=spec,
+        compiler_params=pltpu.CompilerParams(vmem_limit_bytes=VMEM_GRANT),
         name="gram",
     )(received)
     other = lax.ppermute(mine, "dp", [(i, i ^ 1) for i in range(shards)])
-    own_damping = lax.dynamic_slice_in_dim(
-        damping.reshape(-1), lax.axis_index("dp") // owners, 1, 0
-    )
     rows = pl.pallas_call(
         functools.partial(newton_kernel, load_inverse, owners, shards),
-        out_shape=jax.ShapeDtypeStruct((experts_axis, BLOCK // owners, BLOCK), jnp.float32),
+        out_shape=pltpu.VMEM((BLOCK // owners, BLOCK), jnp.float32),
         in_specs=[pl.BlockSpec(memory_space=pltpu.SMEM), spec, spec],
         out_specs=spec,
+        compiler_params=pltpu.CompilerParams(vmem_limit_bytes=VMEM_GRANT),
         name="newton",
-    )(own_damping, mine, other)
-    rows = rows.reshape(experts_axis * BLOCK // owners, BLOCK)
-    gathered = lax.all_to_all(rows, AXES, split_axis=0, concat_axis=0, tiled=True)
-    gathered = gathered.reshape(EXPERTS, FACTORS, NBLK, BLOCK // shards, BLOCK)
-    return gathered[:, 0], gathered[:, 1]
+    )(damping.reshape(-1, FACTORS).T, mine, other)
+    sent = jnp.concatenate([rows.astype(jnp.float16)] * experts_axis, axis=0)
+    gathered = lax.all_to_all(sent, AXES, split_axis=0, concat_axis=0, tiled=True)
+    share = BLOCK // (shards * owners)
+    result = jax.ShapeDtypeStruct((EXPERTS, NBLK, BLOCK // shards, BLOCK), jnp.float32)
+    return pl.pallas_call(
+        functools.partial(decode_kernel, owners, share),
+        out_shape=(result, result),
+        in_specs=[spec],
+        out_specs=(spec, spec),
+        compiler_params=pltpu.CompilerParams(vmem_limit_bytes=VMEM_GRANT),
+        name="decode",
+    )(gathered.astype(jnp.float32))
 
 
 def slot_table(route_ids, capacity):

time: 82 us -> 64.6 us (0.79)
  blocking collectives: 64.4 us -> 51.9 us
  Pallas kernels: 11.6 us -> 6.22 us
  waiting for transfers between devices: 1.42 us -> 2.65 us
  local copies, waits for them, and re-layouts: 3.52 us -> 2.49 us
    all_to_all x1, blocking collectives: 29.8 us -> 17.6 us  [owned(): lax.all_to_all(sent, AXES, split_axis=0, concat_axis=0, tiled=True)]
    pallas_call x2 -> x3, Pallas kernels: 5.47 us -> 2.64 us  [the longest x1 1.33 us: owned(): pl.pallas_call(functools.partial(decode_kernel, owners, share), out_shape...]
    pallas_call x1, Pallas kernels: 6.13 us -> 3.58 us  [owned(): pl.pallas_call(functools.partial(newton_kernel, load_inverse, owners, sha...]
    ppermute x1, waiting for transfers between devices: 1.42 us -> 2.65 us  [owned(): other = lax.ppermute(mine, 'dp', [(i, i ^ 1) for i in range(shards)])]
    unnamed x6 -> x12, local copies, waits for them, and re-layouts: 2.84 us -> 2.49 us
  transfers between devices with their start and end apart: 1 -> 1, of which waited for: 1 -> 1; matrix products, arithmetic and copies ran while one was open for 1% -> 0% of each run, Pallas kernels for 0% -> 0%
where the time goes in v2:
time: 64.6 us; the launch traced here: 64.4 us
  blocking collectives  51.9 us (80%)
  Pallas kernels  6.22 us (10%)
  waiting for transfers between devices  2.65 us (4%)
  local copies, waits for them, and re-layouts  2.49 us (4%)
  between operations  0.72 us (1%)
    all_to_all x1, blocking collectives, owned(): lax.all_to_all(packed, AXES, split_axis=0, concat_axis=0, tiled=True)  34.3 us
    all_to_all x1, blocking collectives, owned(): lax.all_to_all(sent, AXES, split_axis=0, concat_axis=0, tiled=True)  17.6 us
    pallas_call x1, Pallas kernels, owned(): pl.pallas_call(functools.partial(newton_kernel, load_inverse, owners, sha...  3.58 us
    ppermute x1, waiting for transfers between devices, owned(): other = lax.ppermute(mine, 'dp', [(i, i ^ 1) for i in range(shards)])  2.65 us
    unnamed x12, local copies, waits for them, and re-layouts  2.49 us
    pallas_call x1, Pallas kernels, owned(): pl.pallas_call(functools.partial(decode_kernel, owners, share), out_shape...  1.33 us
  transfers between devices with their start and end apart: 1, of which 1 were waited for; matrix products, arithmetic and copies ran while one was open for 0% of the time, Pallas kernels for 0%

profile of v2, /device:TPU:0, one launch (start us, length us, event | category | flops | bytes accessed | tf_op | source)
XLA Modules:
  0.0 64.4 jit_solution(15141925277282948313)
XLA Ops:
  0.6 0.0 copy-start.5
  0.6 0.0 copy-start.2
  0.7 0.0 copy-start.4
  0.7 0.6 copy-done.5
  1.3 0.0 copy-done.2
  1.3 0.0 copy-done.4
  1.3 0.0 copy-start
  1.3 0.9 %copy-done = bf16[128,512]{1,0:T(8,128)(2,1)S(1)} copy-done((bf16[128,512]{1,0:T(8,128)(2,1)S(1)}, bf16[128,512]{1,0:T(8,128)(2,1)}, u32[]{:S(2)}) %copy-start) | copy-done | bytes 131096
  2.2 0.0 copy-start.1
  2.2 0.9 %copy-done.1 = bf16[128,512]{1,0:T(8,128)(2,1)S(1)} copy-done((bf16[128,512]{1,0:T(8,128)(2,1)S(1)}, bf16[128,512]{1,0:T(8,128)(2,1)}, u32[]{:S(2)}) %copy-start.1) | copy-done | bytes 131096
  3.1 0.6 pack.1
  3.7 34.3 %all_to_all.20 = bf16[32,32,512]{2,1,0:T(8,128)(2,1)S(1)} all-to-all(bf16[32,32,512]{2,1,0:T(8,128)(2,1)S(1)} %bitcast.12), channel_id=1, replica_groups=mesh['expert'=2,'dp'=16] {'expert','dp'}, dimensions={0} | all-to-all | bytes 2097152 | tf_op jit(solution)/shard_map/all_to_all | solution.py:189
  38.0 0.7 %gram.1.mine = f32[512,512]{1,0:T(8,128)S(1)} custom-call(bf16[1024,512]{1,0:T(8,128)(2,1)S(1)} %bitcast.13), custom_call_target="tpu_custom_call" | custom-call | tf_op jit(solution)/shard_map/gram/pallas_call | solution.py:190
  38.7 0.0 copy-start.3
  38.8 0.1 collective-permute-start
  38.8 2.6 %collective-permute-done.other = f32[512,512]{1,0:T(8,128)S(1)} collective-permute-done((f32[512,512]{1,0:T(8,128)S(1)}, f32[512,512]{1,0:T(8,128)S(1)}, u32[]{:S(2)}, u32[]{:S(2)}) %collective-permute-start) | collective-permute-done | bytes 1048608 | tf_op jit(solution)/shard_map/ppermute | solution.py:198
  41.5 0.0 copy-done.3
  41.5 3.6 %newton.1 = f32[256,512]{1,0:T(8,128)S(1)} custom-call(f32[2,4]{1,0:T(2,128)S(1)} %bitcast.15, f32[512,512]{1,0:T(8,128)S(1)} %gram.1.mine, f32[512,512]{1,0:T(8,128)S(1)} %collective-permute-done.other), custom_call_target="tpu_custom_call" | custom-call | tf_op jit(solution)/shard_map/newton/pallas_call | solution.py:199
  45.1 0.1 pad_maximum_fusion
  45.2 17.6 %all_to_all.21 = f16[32,16,512]{2,1,0:T(8,128)(2,1)S(1)} all-to-all(f16[32,16,512]{2,1,0:T(8,128)(2,1)S(1)} %bitcast.18), channel_id=1, replica_groups=mesh['expert'=2,'dp'=16] {'expert','dp'}, dimensions={0} | all-to-all | bytes 1048576 | tf_op jit(solution)/shard_map/all_to_all | solution.py:208
  62.9 0.2 bitcast_convert_fusion.rows
  63.0 1.3 %decode.1 = (f32[8,1,32,512]{3,2,1,0:T(8,128)}, f32[8,1,32,512]{3,2,1,0:T(8,128)}) custom-call(f32[512,512]{1,0:T(8,128)S(1)} %bitcast_convert_fusion.rows), custom_call_target="tpu_custom_call" | custom-call | tf_op jit(solution)/shard_map/decode/pallas_call | solution.py:211
  (1 shorter events, 0.0 us)
Async XLA Ops:
  0.6 0.7 %copy-start.5 = (s32[128]{0:T(128)S(1)}, s32[128]{0:T(128)}, u32[]{:S(2)}) copy-start(s32[128]{0:T(128)} %param.10) | copy-start | bytes 1540
  0.6 0.7 %copy-start.2 = (s32[128,2]{0,1:T(2,128)S(1)}, s32[128,2]{0,1:T(2,128)}, u32[]{:S(2)}) copy-start(s32[128,2]{0,1:T(2,128)} %param.8) | copy-start | bytes 3076
  0.7 0.7 %copy-start.4 = (f32[128]{0:T(128)S(1)}, f32[128]{0:T(128)}, u32[]{:S(2)}) copy-start(f32[128]{0:T(128)} %param.9) | copy-start | bytes 1540
  1.3 0.9 %copy-start = (bf16[128,512]{1,0:T(8,128)(2,1)S(1)}, bf16[128,512]{1,0:T(8,128)(2,1)}, u32[]{:S(2)}) copy-start(bf16[128,512]{1,0:T(8,128)(2,1)} %features.1) | copy-start | bytes 393220
  2.2 0.9 %copy-start.1 = (bf16[128,512]{1,0:T(8,128)(2,1)S(1)}, bf16[128,512]{1,0:T(8,128)(2,1)}, u32[]{:S(2)}) copy-start(bf16[128,512]{1,0:T(8,128)(2,1)} %gradients.1) | copy-start | bytes 393220
  38.7 2.7 %copy-start.3 = (f32[4,2,1]{0,2,1:T(1,128)S(1)}, f32[4,2,1]{0,2,1:T(1,128)}, u32[]{:S(2)}) copy-start(f32[4,2,1]{0,2,1:T(1,128)} %param.11) | copy-start | bytes 100
  38.8 2.7 %collective-permute-start = (f32[512,512]{1,0:T(8,128)S(1)}, f32[512,512]{1,0:T(8,128)S(1)}, u32[]{:S(2)}, u32[]{:S(2)}) collective-permute-start(f32[512,512]{1,0:T(8,128)S(1)} %gram.1.mine), channel_id=1, source_target_pairs={{0,1},{1,0},{2,3},{3,2},{4,5},{5,4},{6,7},{7,6},{8,9},{9,8},{10,11... | collective-permute-start | bytes 3145736 | tf_op jit(solution)/shard_map/ppermute | solution.py:198
